TPU v7x, 128 devices: a whole 4x4x4 slice. The times are simulated.
128 devices in a mesh: chan: 4 (over x), az: 8 (over z, y_lo), rng: 4 (over y_hi, core).
Axes of the slice: x: 4, y: 4 (y_hi: 2, y_lo: 2; y = y_hi * 2 + y_lo), z: 4, core: 2. Of those that a mesh axis runs over, the one named last changes fastest.
Arguments:
- raw: float32 [2, 16, 256, 16384], P(None, 'chan', 'rng', 'az'), may hold values from -6 to 6
- taps: float32 [2, 17, 256], P(None, None, 'rng'), may hold values from -1.5 to 1.5
- recon: float32 [2, 16, 16, 16384], P(None, 'az', None, ('chan', 'rng')), may hold values from -1 to 1
- channel_slot: int32 [16], replicated, may hold values from 0 to 15, each once
Outputs:
- reconstructed: float32 [2, 16, 4, 64, 16384], P(None, None, None, 'az', ('chan', 'rng'))
Inputs may be any that keep to these rules, and one draw needn't show every extreme that they name: `channel_slot`: a permutation of the channels.
All inputs are finite; a program needn't handle non-finite values.
Results may differ from a plain program's by a relative error of at most 0.0003.
Values sent between devices are 32-bit elements; how exact they have to be, the bound alone decides.
A program may use at most 192 MiB of HBM per device.

v0:
```python
import functools
import math

import jax
import jax.numpy as jnp
import ml_dtypes
import numpy as np
from jax import lax
from jax.experimental import pallas as pl
from jax.experimental.pallas import tpu as pltpu
from jax.sharding import PartitionSpec as P

MESH = pl.DeviceIdType.MESH
LANES = 128
BF = jnp.bfloat16
F32 = jnp.float32


def tables():
    n = np.arange(LANES)
    angle = 2.0 * np.pi * (np.outer(n, n) % LANES) / LANES
    cos, sin = np.cos(angle), np.sin(angle)
    dft = np.block([[cos, sin], [-sin, cos]])
    turn = 2.0 * np.pi * np.outer(n, n) / (LANES * LANES)
    scale = 1.0 / LANES
    twist = np.stack([np.cos(turn), np.sin(turn)]) * scale
    high = dft.astype(ml_dtypes.bfloat16)
    low = (dft - high.astype(np.float64)).astype(ml_dtypes.bfloat16)
    return np.stack([high, low]), twist.astype(np.float32)


def split(x):
    high = x.astype(BF)
    low = (x - high.astype(F32)).astype(BF)
    return high, low


def product(a, b, dims):
    dot = functools.partial(
        lax.dot_general, dimension_numbers=(dims, ((), ())), preferred_element_type=F32
    )
    return dot(a[0], b[0]) + (dot(a[1], b[0]) + dot(a[0], b[1]))


def kernel(
    raw, taps, recon, slot, dft, twist,
    out,
    xbuf, sbuf, rbuf, ubuf, dbuf, mbuf, acc, band, dftv, twv, tapv,
    load_sem, const_sem, m_ls, halo_ss, halo_rs, a_ss, a_rs, a_ls, m_ss, m_rs,
    c_ss, c_rs, c_ls, out_sem,
):
    ca, aa, ra = lax.axis_index("chan"), lax.axis_index("az"), lax.axis_index("rng")
    n_chan, n_az, n_rng = (lax.axis_size(a) for a in ("chan", "az", "rng"))
    chunks, half = raw.shape[1], (taps.shape[1] - 1) // 2
    rows, width = raw.shape[2], raw.shape[3]
    padded = rows + 2 * half
    group = rows // n_az
    tiles = width // LANES
    az_peers = [lax.rem(aa + d, n_az) for d in range(1, n_az)]
    c_peers = [
        (lax.rem(ca + dc, n_chan), lax.rem(ra + dr, n_rng))
        for dc in range(n_chan) for dr in range(n_rng) if dc or dr
    ]

    loads = [
        pltpu.make_async_copy(raw.at[:, m], xbuf.at[m, :, pl.ds(half, rows)], load_sem.at[m])
        for m in range(chunks)
    ]
    consts = [
        pltpu.make_async_copy(taps, tapv, const_sem.at[0]),
        pltpu.make_async_copy(dft, dftv, const_sem.at[1]),
        pltpu.make_async_copy(twist, twv, const_sem.at[2]),
    ]
    mats = [
        pltpu.make_async_copy(
            recon.at[:, :, :, pl.ds(f * LANES, LANES)], mbuf.at[aa, :, :, f], m_ls.at[f]
        )
        for f in range(group)
    ]
    for cp in [consts[0], loads[0]] + mats + loads[1:] + consts[1:]:
        cp.start()

    barrier = pltpu.get_barrier_semaphore()
    for a in az_peers:
        pl.semaphore_signal(barrier, inc=1, device_id=(ca, a, ra), device_id_type=MESH)
    for c, r in c_peers:
        pl.semaphore_signal(barrier, inc=1, device_id=(c, aa, r), device_id_type=MESH)

    @pl.when(ra == 0)
    def _():
        for m in range(chunks):
            xbuf[m, :, 0:half, :] = jnp.zeros((2, half, width), F32)

    @pl.when(ra == n_rng - 1)
    def _():
        for m in range(chunks):
            xbuf[m, :, padded - half :, :] = jnp.zeros((2, half, width), F32)

    pl.semaphore_wait(barrier, len(az_peers) + len(c_peers))

    def halo(m, side):
        src = raw.at[:, m, pl.ds(rows - half if side == 0 else 0, half)]
        dst = xbuf.at[m, :, pl.ds(0 if side == 0 else padded - half, half)]
        to = lax.rem(ra + (1 if side == 0 else n_rng - 1), n_rng)
        return pltpu.make_async_remote_copy(
            src, dst, halo_ss.at[m, side], halo_rs.at[m, side],
            device_id=(ca, aa, to), device_id_type=MESH,
        )

    for m in range(chunks):
        @pl.when(ra < n_rng - 1)
        def _():
            halo(m, 0).start()

        @pl.when(ra > 0)
        def _():
            halo(m, 1).start()

    pair = aa + 1 - 2 * lax.rem(aa, 2)
    for cp in mats:
        cp.wait()
    to_pair = pltpu.make_async_remote_copy(
        mbuf.at[aa], mbuf.at[aa], m_ss.at[0], m_rs.at[0], device_id=(ca, pair, ra), device_id_type=MESH
    )
    to_pair.start()

    consts[0].wait()
    top = jnp.concatenate([tapv[0], tapv[1]], axis=-1)
    bottom = jnp.concatenate([-tapv[1], tapv[0]], axis=-1)
    lane = lax.broadcasted_iota(jnp.int32, (padded, 2 * rows), 1)
    off = lax.broadcasted_iota(jnp.int32, (padded, 2 * rows), 0) - lax.rem(lane, rows)
    first = jnp.zeros((padded, 2 * rows), F32)
    second = jnp.zeros((padded, 2 * rows), F32)
    for j in range(2 * half + 1):
        hit = off == j
        first = jnp.where(hit, top[j : j + 1, :], first)
        second = jnp.where(hit, bottom[j : j + 1, :], second)
    rest = jnp.zeros((2 * LANES - 2 * padded, 2 * rows), F32)
    matrix = jnp.concatenate([first, second, rest], axis=0).T[:, : 2 * padded]
    high, low = split(matrix)
    band[0] = high
    band[1] = low
    acc[...] = jnp.zeros(acc.shape, F32)

    def a_copy(m, d):
        a = az_peers[d]
        return pltpu.make_async_remote_copy(
            sbuf.at[m, a], rbuf.at[m, :, pl.ds(aa * tiles, tiles)], a_ss.at[m, d], a_rs.at[m, d],
            device_id=(ca, a, ra), device_id_type=MESH,
        )

    def a_local(m):
        return pltpu.make_async_copy(
            sbuf.at[m, aa], rbuf.at[m, :, pl.ds(aa * tiles, tiles)], a_ls.at[m]
        )

    def filtered(m):
        def body(t, carry):
            lanes = pl.ds(pl.multiple_of(t * 2 * LANES, 2 * LANES), 2 * LANES)
            x = jnp.concatenate([xbuf[m, 0, :, lanes], xbuf[m, 1, :, lanes]], axis=0)
            y = product((band[0], band[1]), split(x), ((1,), (0,)))
            for p in range(2):
                for a in range(n_az):
                    at = p * rows + a * group
                    for i in range(2):
                        sbuf[m, a, p, t * 2 + i] = y[at : at + group, i * LANES : (i + 1) * LANES]
            return carry

        lax.fori_loop(0, tiles // 2, body, 0)

    for m in range(chunks):
        loads[m].wait()

        @pl.when(ra > 0)
        def _():
            halo(m, 0).wait_recv()

        @pl.when(ra < n_rng - 1)
        def _():
            halo(m, 1).wait_recv()

        filtered(m)
        for d in range(n_az - 1):
            a_copy(m, d).start()
        a_local(m).start()

    to_pair.wait_recv()

    def m_copy(d, which):
        to = lax.rem(aa + 2 * d, n_az)
        block = aa if which == 0 else pair
        i = 1 + 2 * (d - 1) + which
        return pltpu.make_async_remote_copy(
            mbuf.at[block], mbuf.at[block], m_ss.at[i], m_rs.at[i],
            device_id=(ca, to, ra), device_id_type=MESH,
        )

    passed = [m_copy(d, w) for d in range(1, n_az // 2) for w in range(2)]
    for cp in passed:
        cp.start()

    consts[1].wait()
    consts[2].wait()

    def c_copy(m, i):
        c, r = c_peers[i]
        return pltpu.make_async_remote_copy(
            ubuf.at[m, c * n_rng + r], dbuf.at[m, ca, ra], c_ss.at[m, i], c_rs.at[m, i],
            device_id=(c, aa, r), device_id_type=MESH,
        )

    def c_local(m):
        return pltpu.make_async_copy(ubuf.at[m, ca * n_rng + ra], dbuf.at[m, ca, ra], c_ls.at[m])

    def spectrum(m):
        src = rbuf.reshape(chunks, 2, LANES * group, LANES)
        dst = ubuf.reshape(chunks, n_chan * n_rng, 2, group * group, LANES)

        def body(b, carry):
            q = b * 2
            parts = [
                [src[m, p, pl.ds(q + i, LANES, stride=group), :] for i in range(2)]
                for p in range(2)
            ]
            x = jnp.concatenate([jnp.concatenate(part, axis=1) for part in parts], axis=0)
            y = product((dftv[0], dftv[1]), split(x), ((1,), (0,)))
            turned = []
            for i in range(2):
                re = y[:LANES, i * LANES : (i + 1) * LANES]
                im = y[LANES:, i * LANES : (i + 1) * LANES]
                turned.append(jnp.concatenate(
                    [re * twv[0] + im * twv[1], im * twv[0] - re * twv[1]], axis=1
                ))
            z = product((dftv[0], dftv[1]), split(jnp.concatenate(turned, axis=0)), ((1,), (1,)))
            for p in range(2):
                for to in range(n_chan * n_rng):
                    at = p * LANES + to * group
                    for i in range(2):
                        dst[m, to, p, pl.ds(q + i, group, stride=group), :] = (
                            z[at : at + group, i * LANES : (i + 1) * LANES]
                        )
            return carry

        lax.fori_loop(0, group // 2, body, 0)

    for m in range(chunks):
        a_local(m).wait()
        for d in range(n_az - 1):
            a_copy(m, d).wait_recv()
        spectrum(m)
        for i in range(len(c_peers)):
            c_copy(m, i).start()
        c_local(m).start()

    for cp in passed:
        cp.wait_recv()

    kb = 4

    def reconstruct(m, b):
        k0 = b * kb
        slots = [slot[c * chunks + m] for c in range(n_chan)]

        def body(f, carry):
            lanes = pl.ds(pl.multiple_of(f * LANES, LANES), LANES)
            total = [[[acc[p, k0 + k, s, :, lanes] for s in range(n_rng)] for k in range(kb)]
                     for p in range(2)]
            for c in range(n_chan):
                data = [[dbuf[m, c, s, p, f] for s in range(n_rng)] for p in range(2)]
                for k in range(kb):
                    az, kk = (k0 + k) // 2, k % 2
                    re = mbuf[az, 0, kk, f, pl.ds(slots[c], group, stride=0), :]
                    im = mbuf[az, 1, kk, f, pl.ds(slots[c], group, stride=0), :]
                    for s in range(n_rng):
                        total[0][k][s] = total[0][k][s] + re * data[0][s] - im * data[1][s]
                        total[1][k][s] = total[1][k][s] + re * data[1][s] + im * data[0][s]
            for p in range(2):
                for k in range(kb):
                    for s in range(n_rng):
                        acc[p, k0 + k, s, :, lanes] = total[p][k][s]
            return carry

        lax.fori_loop(0, group, body, 0)

    blocks = acc.shape[1] // kb

    def out_copy(b):
        part = pl.ds(b * kb, kb)
        return pltpu.make_async_copy(acc.at[:, part], out.at[:, part], out_sem.at[b])

    for m in range(chunks):
        c_local(m).wait()
        for i in range(len(c_peers)):
            c_copy(m, i).wait_recv()
        for b in range(blocks):
            reconstruct(m, b)
            if m == chunks - 1:
                out_copy(b).start()

    for m in range(chunks):
        @pl.when(ra < n_rng - 1)
        def _():
            halo(m, 0).wait_send()

        @pl.when(ra > 0)
        def _():
            halo(m, 1).wait_send()

        for d in range(n_az - 1):
            a_copy(m, d).wait_send()
        for i in range(len(c_peers)):
            c_copy(m, i).wait_send()
    to_pair.wait_send()
    for cp in passed:
        cp.wait_send()
    for b in range(blocks):
        out_copy(b).wait()


def shards(raw, taps, recon, channel_slot):
    n_chan, n_az, n_rng = (lax.axis_size(a) for a in ("chan", "az", "rng"))
    chunks, rows, width = raw.shape[1:]
    half = (taps.shape[1] - 1) // 2
    padded = rows + 2 * half
    group, tiles = rows // n_az, width // LANES
    subs, bins = recon.shape[1] * n_az, recon.shape[3]
    dft, twist = tables()
    sem = pltpu.SemaphoreType.DMA
    peers = n_chan * n_rng - 1
    return pl.pallas_call(
        kernel,
        out_shape=jax.ShapeDtypeStruct((2, subs, n_rng, group, bins), F32),
        in_specs=[
            pl.BlockSpec(memory_space=pl.ANY),
            pl.BlockSpec(memory_space=pl.ANY),
            pl.BlockSpec(memory_space=pl.ANY),
            pl.BlockSpec(memory_space=pltpu.SMEM),
            pl.BlockSpec(memory_space=pl.ANY),
            pl.BlockSpec(memory_space=pl.ANY),
        ],
        out_specs=pl.BlockSpec(memory_space=pl.ANY),
        scratch_shapes=[
            pltpu.VMEM((chunks, 2, padded, width), F32),
            pltpu.VMEM((chunks, n_az, 2, tiles, group, LANES), F32),
            pltpu.VMEM((chunks, 2, n_az * tiles, group, LANES), F32),
            pltpu.VMEM((chunks, n_chan * n_rng, 2, group, group, LANES), F32),
            pltpu.VMEM((chunks, n_chan, n_rng, 2, group, group, LANES), F32),
            pltpu.VMEM((n_az, 2, recon.shape[1], bins // LANES, recon.shape[2], LANES), F32),
            pltpu.VMEM((2, subs, n_rng, group, bins), F32),
            pltpu.VMEM((2, 2 * rows, 2 * padded), BF),
            pltpu.VMEM(dft.shape, BF),
            pltpu.VMEM(twist.shape, F32),
            pltpu.VMEM(taps.shape, F32),
            sem((chunks,)),
            sem((3,)),
            sem((bins // LANES,)),
            sem((chunks, 2)),
            sem((chunks, 2)),
            sem((chunks, n_az - 1)),
            sem((chunks, n_az - 1)),
            sem((chunks,)),
            sem((n_az - 1,)),
            sem((n_az - 1,)),
            sem((chunks, peers)),
            sem((chunks, peers)),
            sem((chunks,)),
            sem((subs // 4,)),
        ],
        compiler_params=pltpu.CompilerParams(
            collective_id=0, has_side_effects=True, vmem_limit_bytes=56 * 2**20
        ),
    )(raw, taps, recon, channel_slot, jnp.asarray(dft), jnp.asarray(twist))


def solution(mesh):
    return jax.shard_map(
        shards,
        mesh=mesh,
        in_specs=(
            P(None, "chan", "rng", "az"),
            P(None, None, "rng"),
            P(None, "az", None, ("chan", "rng")),
            P(),
        ),
        out_specs=P(None, None, None, "az", ("chan", "rng")),
        check_vma=False,
    )
```

profile of v0, /device:TPU:1, one launch (start us, length us, event | category | flops | bytes accessed | tf_op | source)
XLA Modules:
  0.0 126.8 jit_solution(13616329405862777154)
XLA Ops:
  0.0 1.3 %copy.7.taps = f32[2,17,64]{2,1,0:T(8,128)} copy(f32[2,17,64]{2,0,1:T(2,128)} %param.7) | data formatting | bytes 17408 | tf_op args[1]
  1.3 120.7 %shard_map.64 = f32[2,16,4,8,1024]{4,3,2,1,0:T(8,128)} custom-call(f32[2,4,64,2048]{3,2,1,0:T(8,128)} %raw.1, f32[2,17,64]{2,1,0:T(8,128)} %copy.7.taps, f32[2,2,16,1024]{3,2,1,0:T(8,128)} %recon.1, s32[16]{0:T(128)} %slot.1, bf16[2,256,256]{2,1,0:T(8,128)(2,1)} %constant.4.clone.dft, f32[2,128,128]{2,1,0:T(8,128)} %constant.5.clone.twist), custom_call_target="tpu_custom_call" | custom-call | tf_op jit(solution)/shard_map/pallas_call | solution.py:330
  122.0 4.8 %copy.9 = f32[2,16,4,8,1024]{4,3,2,1,0:T(8,128)} copy(f32[2,16,4,8,1024]{4,3,2,1,0:T(8,128)} %shard_map.64) | data formatting | bytes 8388608
where the time goes:
time: 127 us
  Pallas kernels  121 us (95%)
  local copies, waits for them, and re-layouts  6.12 us (5%)
    pallas_call x1, Pallas kernels, shards(): pl.pallas_call(kernel, out_shape=jax.ShapeDtypeStruct((2, subs, n_rng, gr...  121 us
    unnamed x2, local copies, waits for them, and re-layouts  6.12 us

commit v1 on v0

--- a/solution.py
+++ b/solution.py
@@ -12,6 +12,8 @@
 
 MESH = pl.DeviceIdType.MESH
 LANES = 128
+KB = 4
+EARLY = 2
 BF = jnp.bfloat16
 F32 = jnp.float32
 
@@ -42,25 +44,73 @@
     return dot(a[0], b[0]) + (dot(a[1], b[0]) + dot(a[0], b[1]))
 
 
+def reconstruct(src, dst, data_ref, mats, sources, slots, first, count):
+    n_rng, _, group = data_ref.shape[1:4]
+
+    def body(at, carry):
+        f, b = lax.rem(at, group), at // group
+        lanes = pl.ds(pl.multiple_of(f * LANES, LANES), LANES)
+        k0 = (first + b) * KB
+        for k in range(KB):
+            total = [[src[p, k0 + k, s, :, lanes] for s in range(n_rng)] for p in range(2)]
+            for c, j in zip(sources, slots):
+                az, kk = (k0 + k) // 2, k % 2
+                re = mats[az, 0, kk, f, pl.ds(j, group, stride=0), :]
+                im = mats[az, 1, kk, f, pl.ds(j, group, stride=0), :]
+                for s in range(n_rng):
+                    x, y = data_ref[c, s, 0, f], data_ref[c, s, 1, f]
+                    total[0][s] = total[0][s] + re * x - im * y
+                    total[1][s] = total[1][s] + re * y + im * x
+            for p in range(2):
+                for s in range(n_rng):
+                    dst[p, k0 + k, s, :, lanes] = total[p][s]
+        return carry
+
+    lax.fori_loop(0, group * count, body, 0)
+
+
+def finish(acc, dlast, mats, slot, out, res, sems):
+    n_chan, subs = dlast.shape[0], acc.shape[1]
+    chunks = slot.shape[0] // n_chan
+    ca = lax.axis_index("chan")
+    late = [lax.rem(ca + n_chan - d, n_chan) for d in range(EARLY, n_chan)]
+    slots = [slot[c * chunks + chunks - 1] for c in late]
+    block = subs // sems.shape[0]
+    copies = []
+    for b in range(sems.shape[0]):
+        reconstruct(acc, res, dlast, mats, late, slots, b * block // KB, block // KB)
+        part = pl.ds(b * block, block)
+        copies.append(pltpu.make_async_copy(res.at[:, part], out.at[:, part], sems.at[b]))
+        copies[b].start()
+    for cp in copies:
+        cp.wait()
+
+
 def kernel(
     raw, taps, recon, slot, dft, twist,
-    out,
-    xbuf, sbuf, rbuf, ubuf, dbuf, mbuf, acc, band, dftv, twv, tapv,
-    load_sem, const_sem, m_ls, halo_ss, halo_rs, a_ss, a_rs, a_ls, m_ss, m_rs,
-    c_ss, c_rs, c_ls, out_sem,
+    acc, dlast, mbuf,
+    xbuf, sbuf, tbuf, rbuf, ubuf, dbuf, band, dftv, twv, tapv,
+    load_sem, const_sem, m_ls, halo_ss, halo_rs, a_ss, a_rs, a_ls, t_ss, t_rs, m_ss, m_rs,
+    c_ss, c_rs, c_ls, ready,
 ):
     ca, aa, ra = lax.axis_index("chan"), lax.axis_index("az"), lax.axis_index("rng")
     n_chan, n_az, n_rng = (lax.axis_size(a) for a in ("chan", "az", "rng"))
-    chunks, half = raw.shape[1], (taps.shape[1] - 1) // 2
+    chunks, half = raw.shape[1], (taps.shape[0] - 1) // 2
     rows, width = raw.shape[2], raw.shape[3]
     padded = rows + 2 * half
     group = rows // n_az
     tiles = width // LANES
     az_peers = [lax.rem(aa + d, n_az) for d in range(1, n_az)]
-    c_peers = [
-        (lax.rem(ca + dc, n_chan), lax.rem(ra + dr, n_rng))
-        for dc in range(n_chan) for dr in range(n_rng) if dc or dr
-    ]
+    core, side_y = lax.rem(ra, 2), ra // 2
+    across = (1 - side_y) * 2
+    chans = [lax.rem(ca + d, n_chan) for d in range(n_chan)]
+    c_peers = [(c, lax.rem(ra + dr, n_rng)) for c in chans for dr in range(n_rng)][1:]
+    pair = aa + 1 - 2 * lax.rem(aa, 2)
+    near = [(ca, pair, ra)]
+    near += [(ca, a, ra) for a in az_peers[1::2]]
+    near += [(ca, aa, across + k) for k in range(2)]
+    near += [(c, aa, side_y * 2 + k) for c in chans[1:] for k in range(2)]
+    near += [(ca, aa, side_y * 2 + 1 - core)]
 
     loads = [
         pltpu.make_async_copy(raw.at[:, m], xbuf.at[m, :, pl.ds(half, rows)], load_sem.at[m])
@@ -81,10 +131,8 @@
         cp.start()
 
     barrier = pltpu.get_barrier_semaphore()
-    for a in az_peers:
-        pl.semaphore_signal(barrier, inc=1, device_id=(ca, a, ra), device_id_type=MESH)
-    for c, r in c_peers:
-        pl.semaphore_signal(barrier, inc=1, device_id=(c, aa, r), device_id_type=MESH)
+    for device in near:
+        pl.semaphore_signal(barrier, inc=1, device_id=device, device_id_type=MESH)
 
     @pl.when(ra == 0)
     def _():
@@ -96,10 +144,10 @@
         for m in range(chunks):
             xbuf[m, :, padded - half :, :] = jnp.zeros((2, half, width), F32)
 
-    pl.semaphore_wait(barrier, len(az_peers) + len(c_peers))
+    pl.semaphore_wait(barrier, len(near))
 
     def halo(m, side):
-        src = raw.at[:, m, pl.ds(rows - half if side == 0 else 0, half)]
+        src = xbuf.at[m, :, pl.ds(rows if side == 0 else half, half)]
         dst = xbuf.at[m, :, pl.ds(0 if side == 0 else padded - half, half)]
         to = lax.rem(ra + (1 if side == 0 else n_rng - 1), n_rng)
         return pltpu.make_async_remote_copy(
@@ -108,6 +156,8 @@
         )
 
     for m in range(chunks):
+        loads[m].wait()
+
         @pl.when(ra < n_rng - 1)
         def _():
             halo(m, 0).start()
@@ -116,7 +166,6 @@
         def _():
             halo(m, 1).start()
 
-    pair = aa + 1 - 2 * lax.rem(aa, 2)
     for cp in mats:
         cp.wait()
     to_pair = pltpu.make_async_remote_copy(
@@ -124,9 +173,12 @@
     )
     to_pair.start()
 
+    for c in chans[1:]:
+        pl.semaphore_signal(ready, inc=1, device_id=(c, aa, ra), device_id_type=MESH)
+
     consts[0].wait()
-    top = jnp.concatenate([tapv[0], tapv[1]], axis=-1)
-    bottom = jnp.concatenate([-tapv[1], tapv[0]], axis=-1)
+    top = jnp.concatenate([tapv[:, 0], tapv[:, 1]], axis=-1)
+    bottom = jnp.concatenate([-tapv[:, 1], tapv[:, 0]], axis=-1)
     lane = lax.broadcasted_iota(jnp.int32, (padded, 2 * rows), 1)
     off = lax.broadcasted_iota(jnp.int32, (padded, 2 * rows), 0) - lax.rem(lane, rows)
     first = jnp.zeros((padded, 2 * rows), F32)
@@ -142,12 +194,37 @@
     band[1] = low
     acc[...] = jnp.zeros(acc.shape, F32)
 
-    def a_copy(m, d):
-        a = az_peers[d]
+    n_z = n_az // 2
+    far = [2, 1, 3]
+
+    def remote(src, dst, send, recv, to):
         return pltpu.make_async_remote_copy(
-            sbuf.at[m, a], rbuf.at[m, :, pl.ds(aa * tiles, tiles)], a_ss.at[m, d], a_rs.at[m, d],
-            device_id=(ca, a, ra), device_id_type=MESH,
-        )
+            src, dst, send, recv, device_id=(ca, to, ra), device_id_type=MESH
+        )
+
+    def along_z(block, d):
+        return lax.rem(block + 2 * d, n_az)
+
+    def spot(m, source):
+        return rbuf.at[m, :, pl.ds(source * tiles, tiles)]
+
+    def z_copy(m, d):
+        to = along_z(aa, d)
+        return remote(sbuf.at[m, to], spot(m, aa), a_ss.at[m, d], a_rs.at[m, d], to)
+
+    def y_copy(m):
+        return remote(sbuf.at[m, pair], spot(m, aa), a_ss.at[m, 0], a_rs.at[m, 0], pair)
+
+    def stage(m, d):
+        src = sbuf.at[m, along_z(pair, d)]
+        return remote(src, tbuf.at[m, d - 1], t_ss.at[m, d - 1], t_rs.at[m, d - 1], pair)
+
+    def forward(m, d):
+        i = n_z + d - 1
+        return remote(tbuf.at[m, d - 1], spot(m, pair), a_ss.at[m, i], a_rs.at[m, i], along_z(aa, d))
+
+    def a_copies(m):
+        return [y_copy(m)] + [f(m, d) for f in (z_copy, forward) for d in far]
 
     def a_local(m):
         return pltpu.make_async_copy(
@@ -169,8 +246,6 @@
         lax.fori_loop(0, tiles // 2, body, 0)
 
     for m in range(chunks):
-        loads[m].wait()
-
         @pl.when(ra > 0)
         def _():
             halo(m, 0).wait_recv()
@@ -180,8 +255,10 @@
             halo(m, 1).wait_recv()
 
         filtered(m)
-        for d in range(n_az - 1):
-            a_copy(m, d).start()
+        for d in far:
+            stage(m, d).start()
+            z_copy(m, d).start()
+        y_copy(m).start()
         a_local(m).start()
 
     to_pair.wait_recv()
@@ -201,16 +278,20 @@
 
     consts[1].wait()
     consts[2].wait()
+    pl.semaphore_wait(ready, n_chan - 1)
+
+    def landing(m):
+        return dlast.at[ca, ra] if m == chunks - 1 else dbuf.at[m, ca, ra]
 
     def c_copy(m, i):
         c, r = c_peers[i]
         return pltpu.make_async_remote_copy(
-            ubuf.at[m, c * n_rng + r], dbuf.at[m, ca, ra], c_ss.at[m, i], c_rs.at[m, i],
+            ubuf.at[m, c * n_rng + r], landing(m), c_ss.at[m, i], c_rs.at[m, i],
             device_id=(c, aa, r), device_id_type=MESH,
         )
 
     def c_local(m):
-        return pltpu.make_async_copy(ubuf.at[m, ca * n_rng + ra], dbuf.at[m, ca, ra], c_ls.at[m])
+        return pltpu.make_async_copy(ubuf.at[m, ca * n_rng + ra], landing(m), c_ls.at[m])
 
     def spectrum(m):
         src = rbuf.reshape(chunks, 2, LANES * group, LANES)
@@ -245,8 +326,11 @@
 
     for m in range(chunks):
         a_local(m).wait()
-        for d in range(n_az - 1):
-            a_copy(m, d).wait_recv()
+        for d in far:
+            stage(m, d).wait_recv()
+            forward(m, d).start()
+        for cp in a_copies(m):
+            cp.wait_recv()
         spectrum(m)
         for i in range(len(c_peers)):
             c_copy(m, i).start()
@@ -255,47 +339,27 @@
     for cp in passed:
         cp.wait_recv()
 
-    kb = 4
-
-    def reconstruct(m, b):
-        k0 = b * kb
-        slots = [slot[c * chunks + m] for c in range(n_chan)]
-
-        def body(f, carry):
-            lanes = pl.ds(pl.multiple_of(f * LANES, LANES), LANES)
-            total = [[[acc[p, k0 + k, s, :, lanes] for s in range(n_rng)] for k in range(kb)]
-                     for p in range(2)]
-            for c in range(n_chan):
-                data = [[dbuf[m, c, s, p, f] for s in range(n_rng)] for p in range(2)]
-                for k in range(kb):
-                    az, kk = (k0 + k) // 2, k % 2
-                    re = mbuf[az, 0, kk, f, pl.ds(slots[c], group, stride=0), :]
-                    im = mbuf[az, 1, kk, f, pl.ds(slots[c], group, stride=0), :]
-                    for s in range(n_rng):
-                        total[0][k][s] = total[0][k][s] + re * data[0][s] - im * data[1][s]
-                        total[1][k][s] = total[1][k][s] + re * data[1][s] + im * data[0][s]
-            for p in range(2):
-                for k in range(kb):
-                    for s in range(n_rng):
-                        acc[p, k0 + k, s, :, lanes] = total[p][k][s]
-            return carry
-
-        lax.fori_loop(0, group, body, 0)
-
-    blocks = acc.shape[1] // kb
-
-    def out_copy(b):
-        part = pl.ds(b * kb, kb)
-        return pltpu.make_async_copy(acc.at[:, part], out.at[:, part], out_sem.at[b])
-
-    for m in range(chunks):
-        c_local(m).wait()
-        for i in range(len(c_peers)):
-            c_copy(m, i).wait_recv()
-        for b in range(blocks):
-            reconstruct(m, b)
-            if m == chunks - 1:
-                out_copy(b).start()
+    def c_wait(m, d):
+        if d == 0:
+            c_local(m).wait()
+        for dr in range(n_rng):
+            if d or dr:
+                c_copy(m, d * n_rng + dr - 1).wait_recv()
+
+    def add(m, ds):
+        for d in ds:
+            c_wait(m, d)
+        sources = [lax.rem(ca + n_chan - d, n_chan) for d in ds]
+        slots = [slot[c * chunks + m] for c in sources]
+        data = dlast if m == chunks - 1 else dbuf.at[m]
+        reconstruct(acc, acc, data, mbuf, sources, slots, 0, acc.shape[1] // KB)
+
+    for m in range(chunks - 1):
+        add(m, range(n_chan))
+    if EARLY:
+        add(chunks - 1, range(EARLY))
+    for d in range(EARLY, n_chan):
+        c_wait(chunks - 1, d)
 
     for m in range(chunks):
         @pl.when(ra < n_rng - 1)
@@ -306,30 +370,34 @@
         def _():
             halo(m, 1).wait_send()
 
-        for d in range(n_az - 1):
-            a_copy(m, d).wait_send()
+        for cp in a_copies(m) + [stage(m, d) for d in far]:
+            cp.wait_send()
         for i in range(len(c_peers)):
             c_copy(m, i).wait_send()
     to_pair.wait_send()
     for cp in passed:
         cp.wait_send()
-    for b in range(blocks):
-        out_copy(b).wait()
 
 
 def shards(raw, taps, recon, channel_slot):
+    taps = jnp.transpose(taps, (1, 0, 2))
     n_chan, n_az, n_rng = (lax.axis_size(a) for a in ("chan", "az", "rng"))
     chunks, rows, width = raw.shape[1:]
-    half = (taps.shape[1] - 1) // 2
+    half = (taps.shape[0] - 1) // 2
     padded = rows + 2 * half
     group, tiles = rows // n_az, width // LANES
     subs, bins = recon.shape[1] * n_az, recon.shape[3]
     dft, twist = tables()
     sem = pltpu.SemaphoreType.DMA
     peers = n_chan * n_rng - 1
-    return pl.pallas_call(
+    vmem = pl.BlockSpec(memory_space=pltpu.VMEM)
+    acc, dlast, mats = pl.pallas_call(
         kernel,
-        out_shape=jax.ShapeDtypeStruct((2, subs, n_rng, group, bins), F32),
+        out_shape=(
+            pltpu.VMEM((2, subs, n_rng, group, bins), F32),
+            pltpu.VMEM((n_chan, n_rng, 2, group, group, LANES), F32),
+            pltpu.VMEM((n_az, 2, recon.shape[1], bins // LANES, recon.shape[2], LANES), F32),
+        ),
         in_specs=[
             pl.BlockSpec(memory_space=pl.ANY),
             pl.BlockSpec(memory_space=pl.ANY),
@@ -338,15 +406,14 @@
             pl.BlockSpec(memory_space=pl.ANY),
             pl.BlockSpec(memory_space=pl.ANY),
         ],
-        out_specs=pl.BlockSpec(memory_space=pl.ANY),
+        out_specs=(vmem, vmem, vmem),
         scratch_shapes=[
             pltpu.VMEM((chunks, 2, padded, width), F32),
             pltpu.VMEM((chunks, n_az, 2, tiles, group, LANES), F32),
+            pltpu.VMEM((chunks, n_az // 2 - 1, 2, tiles, group, LANES), F32),
             pltpu.VMEM((chunks, 2, n_az * tiles, group, LANES), F32),
             pltpu.VMEM((chunks, n_chan * n_rng, 2, group, group, LANES), F32),
-            pltpu.VMEM((chunks, n_chan, n_rng, 2, group, group, LANES), F32),
-            pltpu.VMEM((n_az, 2, recon.shape[1], bins // LANES, recon.shape[2], LANES), F32),
-            pltpu.VMEM((2, subs, n_rng, group, bins), F32),
+            pltpu.VMEM((chunks - 1, n_chan, n_rng, 2, group, group, LANES), F32),
             pltpu.VMEM((2, 2 * rows, 2 * padded), BF),
             pltpu.VMEM(dft.shape, BF),
             pltpu.VMEM(twist.shape, F32),
@@ -359,17 +426,27 @@
             sem((chunks, n_az - 1)),
             sem((chunks, n_az - 1)),
             sem((chunks,)),
+            sem((chunks, n_az // 2 - 1)),
+            sem((chunks, n_az // 2 - 1)),
             sem((n_az - 1,)),
             sem((n_az - 1,)),
             sem((chunks, peers)),
             sem((chunks, peers)),
             sem((chunks,)),
-            sem((subs // 4,)),
+            pltpu.SemaphoreType.REGULAR,
         ],
         compiler_params=pltpu.CompilerParams(
-            collective_id=0, has_side_effects=True, vmem_limit_bytes=56 * 2**20
+            collective_id=0, has_side_effects=True, vmem_limit_bytes=52 * 2**20
         ),
     )(raw, taps, recon, channel_slot, jnp.asarray(dft), jnp.asarray(twist))
+    return pl.pallas_call(
+        finish,
+        out_shape=jax.ShapeDtypeStruct((2, subs, n_rng, group, bins), F32),
+        in_specs=[vmem, vmem, vmem, pl.BlockSpec(memory_space=pltpu.SMEM)],
+        out_specs=pl.BlockSpec(memory_space=pl.ANY),
+        scratch_shapes=[pltpu.VMEM((2, subs, n_rng, group, bins), F32), sem((subs // 4,))],
+        compiler_params=pltpu.CompilerParams(vmem_limit_bytes=16 * 2**20),
+    )(acc, dlast, mats, channel_slot)
 
 
 def solution(mesh):

time: 127 us -> 121 us (0.953)
  local copies, waits for them, and re-layouts: 6.12 us -> 0.01 us
    unnamed x2, local copies, waits for them, and re-layouts: 6.12 us -> 0.01 us
    pallas_call x1 -> x2, Pallas kernels: 121 us -> 120 us  [the longest x1 116 us: shards(): pl.pallas_call(kernel, out_shape=(pltpu.VMEM((2, subs, n_rng, group, bins...]
where the time goes in v1:
time: 121 us; the launch traced here: 120 us
  Pallas kernels  120 us (99%)
    pallas_call x1, Pallas kernels, shards(): pl.pallas_call(kernel, out_shape=(pltpu.VMEM((2, subs, n_rng, group, bins...  116 us
    pallas_call x1, Pallas kernels, shards(): pl.pallas_call(finish, out_shape=jax.ShapeDtypeStruct((2, subs, n_rng, gr...  3.31 us

profile of v1, /device:TPU:1, one launch (start us, length us, event | category | flops | bytes accessed | tf_op | source)
XLA Modules:
  0.0 119.6 jit_solution(14551602717188577657)
XLA Ops:
  0.0 0.0 copy-start
  0.0 116.2 %shard_map.64 = (f32[2,16,4,8,1024]{4,3,2,1,0:T(8,128)S(1)}, f32[4,4,2,8,8,128]{5,4,3,2,1,0:T(8,128)S(1)}, f32[8,2,2,8,16,128]{5,4,3,2,1,0:T(8,128)S(1)}) custom-call(f32[2,4,64,2048]{3,2,1,0:T(8,128)} %raw.1, f32[17,2,64]{2,1,0:T(2,128)} %bitcast.1, f32[2,2,16,1024]{3,2,1,0:T(8,128)} %recon.1, s32[16]{0:T(128)} %slot.3, ...), custom_call_target="tpu_custom_call" | custom-call | tf_op jit(solution)/shard_map/pallas_call | solution.py:394
  116.3 0.0 copy-done
  116.3 3.3 %shard_map.65 = f32[2,16,4,8,1024]{4,3,2,1,0:T(8,128)} custom-call(f32[2,16,4,8,1024]{4,3,2,1,0:T(8,128)S(1)} %get-tuple-element.8.acc, f32[4,4,2,8,8,128]{5,4,3,2,1,0:T(8,128)S(1)} %get-tuple-element.9.dlast, f32[8,2,2,8,16,128]{5,4,3,2,1,0:T(8,128)S(1)} %get-tuple-element.10.mats, s32[16]{0:T(128)S(1)} %copy-done), custom_call_target="tpu_custom_call" | custom-call | tf_op jit(solution)/shard_map/pallas_call | solution.py:442
Async XLA Ops:
  0.0 116.3 %copy-start = (s32[16]{0:T(128)S(1)}, s32[16]{0:T(128)}, u32[]{:S(2)}) copy-start(s32[16]{0:T(128)} %slot.3) | copy-start | bytes 196

commit v2 on v1

--- a/solution.py
+++ b/solution.py
@@ -14,6 +14,7 @@
 LANES = 128
 KB = 4
 EARLY = 2
+ORDER = (0, 2, 1, 3)
 BF = jnp.bfloat16
 F32 = jnp.float32
 
@@ -73,7 +74,7 @@
     n_chan, subs = dlast.shape[0], acc.shape[1]
     chunks = slot.shape[0] // n_chan
     ca = lax.axis_index("chan")
-    late = [lax.rem(ca + n_chan - d, n_chan) for d in range(EARLY, n_chan)]
+    late = [lax.rem(ca + n_chan - d, n_chan) for d in ORDER[EARLY:]]
     slots = [slot[c * chunks + chunks - 1] for c in late]
     block = subs // sems.shape[0]
     copies = []
@@ -104,7 +105,7 @@
     core, side_y = lax.rem(ra, 2), ra // 2
     across = (1 - side_y) * 2
     chans = [lax.rem(ca + d, n_chan) for d in range(n_chan)]
-    c_peers = [(c, lax.rem(ra + dr, n_rng)) for c in chans for dr in range(n_rng)][1:]
+    c_peers = [(c, lax.rem(ra + dr, n_rng)) for c in [chans[d] for d in ORDER] for dr in range(n_rng)][1:]
     pair = aa + 1 - 2 * lax.rem(aa, 2)
     near = [(ca, pair, ra)]
     near += [(ca, a, ra) for a in az_peers[1::2]]
@@ -292,6 +293,11 @@
 
     def c_local(m):
         return pltpu.make_async_copy(ubuf.at[m, ca * n_rng + ra], landing(m), c_ls.at[m])
+
+    def c_start(m):
+        for i in range(len(c_peers)):
+            c_copy(m, i).start()
+        c_local(m).start()
 
     def spectrum(m):
         src = rbuf.reshape(chunks, 2, LANES * group, LANES)
@@ -329,12 +335,13 @@
         for d in far:
             stage(m, d).wait_recv()
             forward(m, d).start()
+        if m:
+            c_start(m - 1)
         for cp in a_copies(m):
             cp.wait_recv()
         spectrum(m)
-        for i in range(len(c_peers)):
-            c_copy(m, i).start()
-        c_local(m).start()
+        if m == chunks - 1:
+            c_start(m)
 
     for cp in passed:
         cp.wait_recv()
@@ -349,7 +356,7 @@
     def add(m, ds):
         for d in ds:
             c_wait(m, d)
-        sources = [lax.rem(ca + n_chan - d, n_chan) for d in ds]
+        sources = [lax.rem(ca + n_chan - ORDER[d], n_chan) for d in ds]
         slots = [slot[c * chunks + m] for c in sources]
         data = dlast if m == chunks - 1 else dbuf.at[m]
         reconstruct(acc, acc, data, mbuf, sources, slots, 0, acc.shape[1] // KB)

time: 121 us -> 120 us (level)
  no operation moved by 1% of the time
where the time goes in v2:
time: 120 us
  Pallas kernels  120 us (100%)
    pallas_call x1, Pallas kernels, shards(): pl.pallas_call(kernel, out_shape=(pltpu.VMEM((2, subs, n_rng, group, bins...  116 us
    pallas_call x1, Pallas kernels, shards(): pl.pallas_call(finish, out_shape=jax.ShapeDtypeStruct((2, subs, n_rng, gr...  3.31 us

profile of v2, /device:TPU:1, one launch (start us, length us, event | category | flops | bytes accessed | tf_op | source)
XLA Modules:
  0.0 119.6 jit_solution(3080951118825575026)
XLA Ops:
  0.0 0.0 copy-start
  0.0 116.3 %shard_map.64 = (f32[2,16,4,8,1024]{4,3,2,1,0:T(8,128)S(1)}, f32[4,4,2,8,8,128]{5,4,3,2,1,0:T(8,128)S(1)}, f32[8,2,2,8,16,128]{5,4,3,2,1,0:T(8,128)S(1)}) custom-call(f32[2,4,64,2048]{3,2,1,0:T(8,128)} %raw.1, f32[17,2,64]{2,1,0:T(2,128)} %bitcast.1, f32[2,2,16,1024]{3,2,1,0:T(8,128)} %recon.1, s32[16]{0:T(128)} %slot.3, ...), custom_call_target="tpu_custom_call" | custom-call | tf_op jit(solution)/shard_map/pallas_call | solution.py:401
  116.3 0.0 copy-done
  116.3 3.3 %shard_map.65 = f32[2,16,4,8,1024]{4,3,2,1,0:T(8,128)} custom-call(f32[2,16,4,8,1024]{4,3,2,1,0:T(8,128)S(1)} %get-tuple-element.8.acc, f32[4,4,2,8,8,128]{5,4,3,2,1,0:T(8,128)S(1)} %get-tuple-element.9.dlast, f32[8,2,2,8,16,128]{5,4,3,2,1,0:T(8,128)S(1)} %get-tuple-element.10.mats, s32[16]{0:T(128)S(1)} %copy-done), custom_call_target="tpu_custom_call" | custom-call | tf_op jit(solution)/shard_map/pallas_call | solution.py:449
Async XLA Ops:
  0.0 116.3 %copy-start = (s32[16]{0:T(128)S(1)}, s32[16]{0:T(128)}, u32[]{:S(2)}) copy-start(s32[16]{0:T(128)} %slot.3) | copy-start | bytes 196
